TPU v7x, 32 devices: a whole 2x2x4 slice. The times are simulated.
32 devices in a mesh: dp: 4 (over z), row: 4 (over y, x), col: 2 (over core).
Axes of the slice: x: 2, y: 2, z: 4, core: 2. Of those that a mesh axis runs over, the one named last changes fastest.
Arguments:
- tokens: bfloat16 [4096, 1600], P(('dp', 'row'), 'col'), may hold values from -6 to 6
- segment_ids: int32 [4, 1024], P('dp'), may hold values from 0 to 3, as said below
- first_gain: float32 [1600], replicated, may hold values from 0.1 to 1.9
- first_shift: float32 [1600], replicated, may hold values from -3 to 3
- triple_weight: bfloat16 [1600, 4800], P('col', 'row'), may hold values from -1 to 1
- query_bias: float32 [1600], replicated, may hold values from -3 to 3
- value_bias: float32 [1600], replicated, may hold values from -3 to 3
- proj_weight: bfloat16 [1600, 1600], P('row', 'col'), may hold values from -0.4375 to 0.4375
- proj_bias: float32 [1600], replicated, may hold values from -3 to 3
- second_gain: float32 [1600], replicated, may hold values from 0.1 to 1.9
- second_shift: float32 [1600], replicated, may hold values from -3 to 3
- expand_weight: bfloat16 [1600, 6400], P('col', 'row'), may hold values from -0.15625 to 0.15625
- expand_bias: float32 [6400], replicated, may hold values from -3 to 3
- shrink_weight: bfloat16 [6400, 1600], P('row', 'col'), may hold values from -0.078125 to 0.078125
- shrink_bias: float32 [1600], replicated, may hold values from -3 to 3
- cotangent: bfloat16 [4096, 1600], P(('dp', 'row'), 'col'), may hold values from -6 to 6
Outputs:
- block_out: bfloat16 [4096, 1600], P(('dp', 'row'), 'col')
- input_grad: float32 [4096, 1600], P(('dp', 'row'), 'col')
- first_gain_grad: float32 [1600], replicated
- first_shift_grad: float32 [1600], replicated
- triple_grad: float32 [2, 800, 4800], P('col', 'dp', 'row')
- query_bias_grad: float32 [1600], replicated
- value_bias_grad: float32 [1600], replicated
- proj_grad: float32 [4, 400, 1600], P('row', 'dp', 'col')
- proj_bias_grad: float32 [1600], replicated
- second_gain_grad: float32 [1600], replicated
- second_shift_grad: float32 [1600], replicated
- expand_grad: float32 [2, 800, 6400], P('col', 'dp', 'row')
- expand_bias_grad: float32 [6400], replicated
- shrink_grad: float32 [4, 1600, 1600], P('row', 'dp', 'col')
- shrink_bias_grad: float32 [1600], replicated
Inputs may be any that keep to these rules, and one draw needn't show every extreme that they name: `segment_ids`: each row lists the sequences of one data group in order: it starts at 0 and rises by one where a new sequence starts. A row holds 1 to 4 sequences; in every draw some row holds exactly 4 and another holds a single sequence of 1024 tokens.
All inputs are finite; a program needn't handle non-finite values.
Results may differ from a plain program's by a relative error of at most 0.014.
Values may be sent and summed in bfloat16 or wider, within the bound.
A program may use at most 192 MiB of HBM per device.

v0:
```python
import math
import jax
import jax.numpy as jnp
from jax import lax
from jax.sharding import PartitionSpec as P

HEADS = 25
HEAD_DIM = 64
FF = 6400
EPS = 1e-05
NEG = -1e30


def gelu_tanh(values):
    return (
        0.5
        * values
        * (1.0 + jnp.tanh(0.7978845608028654 * (values + 0.044715 * values * values * values)))
    )


def spread_rows(own_part):
    return lax.all_gather(own_part, "row", axis=0, tiled=True)


def reduce_cols(partial_sum):
    return lax.psum_scatter(partial_sum, "col", scatter_dimension=0, tiled=True)


def spread_cols(own_part):
    return lax.all_gather(own_part, "col", axis=0, tiled=True)


def reduce_rows(partial_sum):
    return lax.psum_scatter(partial_sum, "row", scatter_dimension=0, tiled=True)


def to_heads(hidden):
    return lax.all_to_all(hidden, "row", split_axis=0, concat_axis=1, tiled=True)


def to_hidden(headed):
    return lax.all_to_all(headed, "row", split_axis=1, concat_axis=0, tiled=True)


def gather_keys(own_part):
    return lax.all_gather(own_part, ("row", "col"), axis=0, tiled=True)


def feature_totals(first_term, second_term):
    return lax.psum(
        (jnp.sum(first_term, axis=1, keepdims=True), jnp.sum(second_term, axis=1, keepdims=True)),
        "col",
    )


def norm_local(matrix, gain, shift):
    width = HEADS * HEAD_DIM
    total, square = feature_totals(matrix, matrix * matrix)
    average = total / width
    rstd = lax.rsqrt(square / width - average * average + EPS)
    normed_hat = (matrix - average) * rstd
    return (normed_hat * gain + shift, normed_hat, rstd)


def norm_back(grad_in, normed_hat, rstd, gain):
    width = HEADS * HEAD_DIM
    scaled = grad_in * gain
    total, mixed = feature_totals(scaled, scaled * normed_hat)
    return rstd * (scaled - total / width - normed_hat * mixed / width)


def head_split(matrix):
    rows = matrix.shape[0]
    group_size = math.gcd(HEADS, 5)
    return matrix.reshape(rows, HEADS // group_size, group_size, HEAD_DIM).transpose(1, 0, 2, 3)


def head_join(blocks):
    rows = blocks.shape[1]
    return blocks.transpose(1, 0, 2, 3).reshape(rows, HEADS * HEAD_DIM)


def attention_forward(query_part, key_part, value_part, allowed):
    scaling = HEAD_DIM ** (-0.5)

    def one_group(blocks):
        query_block, key_block, value_block = blocks
        scores = (
            jnp.einsum("qhd,khd->hqk", query_block, key_block, preferred_element_type=jnp.float32)
            * scaling
        )
        scores = jnp.where(allowed[None], scores, NEG)
        highest = jnp.max(scores, axis=-1)
        log_total = highest + jnp.log(jnp.sum(jnp.exp(scores - highest[..., None]), axis=-1))
        weights = jnp.exp(scores - log_total[..., None]).astype(jnp.bfloat16)
        combined = jnp.einsum(
            "hqk,khd->qhd", weights, value_block, preferred_element_type=jnp.float32
        ).astype(jnp.bfloat16)
        return (combined, log_total)

    combined, log_total = lax.map(
        one_group, (head_split(query_part), head_split(key_part), head_split(value_part))
    )
    return (head_join(combined), log_total)


def attention_backward(
    query_part, key_part, value_part, attended, attended_grad, log_total, allowed
):
    scaling = HEAD_DIM ** (-0.5)

    def one_group(blocks):
        query_block, key_block, value_block, out_block, grad_block, lse_block = blocks
        scores = (
            jnp.einsum("qhd,khd->hqk", query_block, key_block, preferred_element_type=jnp.float32)
            * scaling
        )
        scores = jnp.where(allowed[None], scores, NEG)
        weights = jnp.exp(scores - lse_block[..., None])
        weights_half = weights.astype(jnp.bfloat16)
        value_grad = jnp.einsum(
            "hqk,qhd->khd", weights_half, grad_block, preferred_element_type=jnp.float32
        )
        weight_grad = jnp.einsum(
            "qhd,khd->hqk", grad_block, value_block, preferred_element_type=jnp.float32
        )
        delta = jnp.sum(
            grad_block.astype(jnp.float32) * out_block.astype(jnp.float32), axis=-1
        ).transpose(1, 0)
        mix_half = (weights * (weight_grad - delta[..., None])).astype(jnp.bfloat16)
        query_grad = (
            jnp.einsum("hqk,khd->qhd", mix_half, key_block, preferred_element_type=jnp.float32)
            * scaling
        )
        key_grad = (
            jnp.einsum("hqk,qhd->khd", mix_half, query_block, preferred_element_type=jnp.float32)
            * scaling
        )
        return (query_grad, key_grad, value_grad)

    query_grad, key_grad, value_grad = lax.map(
        one_group,
        (
            head_split(query_part),
            head_split(key_part),
            head_split(value_part),
            head_split(attended),
            head_split(attended_grad),
            log_total,
        ),
    )
    return (head_join(query_grad), head_join(key_grad), head_join(value_grad))


def shards(
    tokens,
    segment_ids,
    first_gain,
    first_shift,
    triple_weight,
    query_bias,
    value_bias,
    proj_weight,
    proj_bias,
    second_gain,
    second_shift,
    expand_weight,
    expand_bias,
    shrink_weight,
    shrink_bias,
    cotangent,
):
    width = HEADS * HEAD_DIM
    row_count = lax.axis_size("row")
    col_count = lax.axis_size("col")
    row_index = lax.axis_index("row")
    col_index = lax.axis_index("col")
    col_width = tokens.shape[1]
    group_rows = segment_ids.shape[1]
    query_rows = group_rows // (row_count * col_count)
    hidden_width = expand_weight.shape[1]
    triple_width = triple_weight.shape[1]

    def col_slice(vector):
        return lax.dynamic_slice_in_dim(vector, col_index * col_width, col_width)

    def col_place(vector):
        return lax.dynamic_update_slice_in_dim(
            jnp.zeros((width,), jnp.float32), vector, col_index * col_width, 0
        )

    tokens_wide = tokens.astype(jnp.float32)
    first_normed, first_hat, first_rstd = norm_local(
        tokens_wide, col_slice(first_gain), col_slice(first_shift)
    )
    first_half = first_normed.astype(jnp.bfloat16)
    first_all = spread_rows(first_half)
    full_bias = jnp.concatenate([query_bias, jnp.zeros((width,), jnp.float32), value_bias])
    triple_sum = reduce_cols(jnp.dot(first_all, triple_weight, preferred_element_type=jnp.float32))
    triple_local = (
        triple_sum + lax.dynamic_slice_in_dim(full_bias, row_index * triple_width, triple_width)
    ).astype(jnp.bfloat16)
    headed = to_heads(triple_local)
    query_part = headed[:, :width]
    pair_local = headed[:, width:]
    pair_all = gather_keys(pair_local)
    segment_row = segment_ids[0]
    query_start = col_index * (group_rows // col_count) + row_index * query_rows
    query_places = query_start + jnp.arange(query_rows, dtype=jnp.int32)
    query_segments = lax.dynamic_slice_in_dim(segment_row, query_start, query_rows)
    key_places = (
        jnp.arange(group_rows, dtype=jnp.int32)
        .reshape(col_count, row_count, query_rows)
        .transpose(1, 0, 2)
        .reshape(group_rows)
    )
    key_segments = (
        segment_row.reshape(col_count, row_count, query_rows).transpose(1, 0, 2).reshape(group_rows)
    )
    allowed = (query_segments[:, None] == key_segments[None, :]) & (
        key_places[None, :] <= query_places[:, None]
    )
    attended, log_total = attention_forward(
        query_part, pair_all[:, :width], pair_all[:, width:], allowed
    )
    attended_hidden = to_hidden(attended)
    attended_all = spread_cols(attended_hidden)
    middle = (
        tokens_wide
        + reduce_rows(jnp.dot(attended_all, proj_weight, preferred_element_type=jnp.float32))
        + col_slice(proj_bias)
    )
    second_normed, second_hat, second_rstd = norm_local(
        middle, col_slice(second_gain), col_slice(second_shift)
    )
    second_half = second_normed.astype(jnp.bfloat16)
    second_all = spread_rows(second_half)
    before_act = reduce_cols(
        jnp.dot(second_all, expand_weight, preferred_element_type=jnp.float32)
    ) + lax.dynamic_slice_in_dim(expand_bias, row_index * hidden_width, hidden_width)
    activated = gelu_tanh(before_act).astype(jnp.bfloat16)
    activated_all = spread_cols(activated)
    block_out = (
        middle
        + reduce_rows(jnp.dot(activated_all, shrink_weight, preferred_element_type=jnp.float32))
        + col_slice(shrink_bias)
    ).astype(jnp.bfloat16)
    pair_back = gather_keys(pair_local)
    activated_back = spread_cols(activated)
    second_back = spread_rows(second_half)
    attended_back = spread_cols(attended_hidden)
    first_back = spread_rows(first_half)
    cot_wide = cotangent.astype(jnp.float32)
    cot_all = spread_rows(cotangent)
    shrink_grad = jnp.einsum(
        "tf,td->fd", activated_back, cot_all, preferred_element_type=jnp.float32
    )
    shrink_bias_part = jnp.sum(cot_wide, axis=0)
    act_grad = reduce_cols(
        jnp.einsum("td,fd->tf", cot_all, shrink_weight, preferred_element_type=jnp.float32)
    )
    gelu_back = jax.vjp(gelu_tanh, before_act)[1]
    before_grad = gelu_back(act_grad)[0]
    expand_bias_part = jnp.sum(before_grad, axis=0)
    hidden_grad = before_grad.astype(jnp.bfloat16)
    hidden_all = spread_cols(hidden_grad)
    expand_grad = jnp.einsum(
        "td,tf->df", second_back, hidden_all, preferred_element_type=jnp.float32
    )
    second_normed_grad = reduce_rows(
        jnp.einsum("tf,df->td", hidden_all, expand_weight, preferred_element_type=jnp.float32)
    )
    middle_grad = cot_wide + norm_back(
        second_normed_grad, second_hat, second_rstd, col_slice(second_gain)
    )
    second_gain_part = jnp.sum(second_normed_grad * second_hat, axis=0)
    second_shift_part = jnp.sum(second_normed_grad, axis=0)
    middle_half = middle_grad.astype(jnp.bfloat16)
    middle_all = spread_rows(middle_half)
    proj_grad = jnp.einsum(
        "tc,td->cd", attended_back, middle_all, preferred_element_type=jnp.float32
    )
    proj_bias_part = jnp.sum(middle_grad, axis=0)
    attended_grad_hidden = reduce_cols(
        jnp.einsum("td,cd->tc", middle_all, proj_weight, preferred_element_type=jnp.float32)
    ).astype(jnp.bfloat16)
    attended_grad = to_heads(attended_grad_hidden)
    query_grad, key_grad, value_grad = attention_backward(
        query_part,
        pair_back[:, :width],
        pair_back[:, width:],
        attended,
        attended_grad,
        log_total,
        allowed,
    )
    pair_grad = lax.psum_scatter(
        jnp.concatenate([key_grad, value_grad], axis=1).astype(jnp.bfloat16),
        ("row", "col"),
        scatter_dimension=0,
        tiled=True,
    ).astype(jnp.float32)
    query_bias_part = jnp.sum(query_grad, axis=0)
    value_bias_part = jnp.sum(pair_grad[:, width:], axis=0)
    triple_half = jnp.concatenate([query_grad, pair_grad], axis=1).astype(jnp.bfloat16)
    triple_hidden = to_hidden(triple_half)
    triple_all = spread_cols(triple_hidden)
    triple_grad = jnp.einsum(
        "tc,tk->ck", first_back, triple_all, preferred_element_type=jnp.float32
    )
    first_normed_grad = reduce_rows(
        jnp.einsum("tk,ck->tc", triple_all, triple_weight, preferred_element_type=jnp.float32)
    )
    input_grad = middle_grad + norm_back(
        first_normed_grad, first_hat, first_rstd, col_slice(first_gain)
    )
    first_gain_part = jnp.sum(first_normed_grad * first_hat, axis=0)
    first_shift_part = jnp.sum(first_normed_grad, axis=0)
    shrink_owned, expand_owned, proj_owned, triple_owned = (
        lax.psum_scatter(
            shrink_grad.astype(jnp.bfloat16), "dp", scatter_dimension=0, tiled=True
        ).astype(jnp.float32),
        lax.psum_scatter(
            expand_grad.astype(jnp.bfloat16), "dp", scatter_dimension=0, tiled=True
        ).astype(jnp.float32),
        lax.psum_scatter(
            proj_grad.astype(jnp.bfloat16), "dp", scatter_dimension=0, tiled=True
        ).astype(jnp.float32),
        lax.psum_scatter(
            triple_grad.astype(jnp.bfloat16), "dp", scatter_dimension=0, tiled=True
        ).astype(jnp.float32),
    )
    expand_bias_full = lax.dynamic_update_slice_in_dim(
        jnp.zeros((FF,), jnp.float32), expand_bias_part, row_index * hidden_width, 0
    )
    (
        first_gain_grad,
        first_shift_grad,
        query_bias_grad,
        value_bias_grad,
        proj_bias_grad,
        second_gain_grad,
        second_shift_grad,
        expand_bias_grad,
        shrink_bias_grad,
    ) = lax.psum(
        (
            col_place(first_gain_part),
            col_place(first_shift_part),
            query_bias_part,
            value_bias_part,
            col_place(proj_bias_part),
            col_place(second_gain_part),
            col_place(second_shift_part),
            expand_bias_full,
            col_place(shrink_bias_part),
        ),
        ("dp", "row", "col"),
    )
    return (
        block_out,
        input_grad,
        first_gain_grad,
        first_shift_grad,
        triple_owned[None],
        query_bias_grad,
        value_bias_grad,
        proj_owned[None],
        proj_bias_grad,
        second_gain_grad,
        second_shift_grad,
        expand_owned[None],
        expand_bias_grad,
        shrink_owned[None],
        shrink_bias_grad,
    )


def solution(mesh):
    in_specs = (
        P(("dp", "row"), "col"),
        P("dp", None),
        P(),
        P(),
        P("col", "row"),
        P(),
        P(),
        P("row", "col"),
        P(),
        P(),
        P(),
        P("col", "row"),
        P(),
        P("row", "col"),
        P(),
        P(("dp", "row"), "col"),
    )
    out_specs = (
        P(("dp", "row"), "col"),
        P(("dp", "row"), "col"),
        P(),
        P(),
        P("col", "dp", "row"),
        P(),
        P(),
        P("row", "dp", "col"),
        P(),
        P(),
        P(),
        P("col", "dp", "row"),
        P(),
        P("row", "dp", "col"),
        P(),
    )
    return jax.shard_map(shards, mesh=mesh, in_specs=in_specs, out_specs=out_specs, check_vma=False)
```

profile of v0, /device:TPU:8, one launch (start us, length us, event | category | flops | bytes accessed | tf_op | source)
XLA Modules:
  0.0 1063.2 jit_solution(4812785820477544003)
XLA Ops:
  14.7 32.5 %all-gather.9.cloned.1.call-done = bf16[1024,800]{0,1:T(8,128)(2,1)} async-done(((bf16[256,800]{0,1:T(8,128)(2,1)}), bf16[1024,800]{0,1:T(8,128)(2,1)}) %all-gather.9.cloned.1.call-update) | async-done | bytes 1638416 | tf_op jit(solution)/shard_map/all_gather | solution.py:23
  55.1 12.2 %reduce-scatter.19.cloned.1.call-done = f32[512,1200]{0,1:T(8,128)} async-done(((f32[1024,1200]{0,1:T(8,128)}), f32[512,1200]{0,1:T(8,128)}) %reduce-scatter.19.cloned.1.call-update) | async-done | bytes 2457616 | tf_op jit(solution)/shard_map/reduce_scatter | solution.py:27
  69.2 20.1 %all_to_all.70 = bf16[4,128,1200]{1,2,0:T(8,128)(2,1)S(1)} all-to-all(bf16[4,128,1200]{1,2,0:T(8,128)(2,1)S(1)} %copy_bitcast_fusion.1), channel_id=1, replica_groups=mesh['dp'=4,'row'=4,'col'=2] {'row'}, dimensions={0} | all-to-all | bytes 2457600 | tf_op jit(solution)/shard_map/all_to_all | solution.py:39
  92.5 45.9 %all-gather.11.cloned.1.call-done = bf16[1024,3200]{0,1:T(8,128)(2,1)} async-done(((bf16[128,3200]{0,1:T(8,128)(2,1)}), bf16[1024,3200]{0,1:T(8,128)(2,1)}) %all-gather.11.cloned.1.call-update) | async-done | bytes 6553616 | tf_op jit(solution)/shard_map/all_gather | solution.py:47
  144.8 23.5 %while.28 = (s32[]{:T(128)}, bf16[5,128,5,64]{1,3,2,0:T(8,128)(2,1)S(1)}, f32[5,5,128]{2,1,0:T(8,128)S(1)}, bf16[5,1024,5,64]{1,3,2,0:T(8,128)(2,1)}, bf16[5,128...) while((s32[]{:T(128)}, ...), condition=%wide.region_8.9_spmd.clone, body=%wide.region_5.8_spmd.clone.sunk | while | flops 175414656 | bytes 9902713 | solution.py:102
  168.3 10.8 %all_to_all.71 = bf16[128,4,400]{0,2,1:T(8,128)(2,1)S(1)} all-to-all(bf16[128,4,400]{0,2,1:T(8,128)(2,1)S(1)} %bitcast.232), channel_id=1, replica_groups=mesh['dp'=4,'row'=4,'col'=2] {'row'}, dimensions={1} | all-to-all | bytes 819200 | tf_op jit(solution)/shard_map/all_to_all | solution.py:43
  186.1 43.4 %reduce-scatter.21.cloned.1.call-done = f32[256,800]{0,1:T(8,128)} async-done(((f32[1024,800]{0,1:T(8,128)}), f32[256,800]{0,1:T(8,128)}) %reduce-scatter.21.cloned.1.call-update) | async-done | bytes 819216 | tf_op jit(solution)/shard_map/reduce_scatter | solution.py:35
  236.2 26.2 %all-gather.17.cloned.1.call-done = bf16[1024,800]{0,1:T(8,128)(2,1)} async-done(((bf16[256,800]{0,1:T(8,128)(2,1)}), bf16[1024,800]{0,1:T(8,128)(2,1)}) %all-gather.17.cloned.1.call-update) | async-done | bytes 1638416 | tf_op jit(solution)/shard_map/all_gather | solution.py:23
  271.0 24.9 %all-gather.13.cloned.1.call-done = bf16[1024,800]{0,1:T(8,128)(2,1)} async-done(((bf16[256,800]{0,1:T(8,128)(2,1)}), bf16[1024,800]{0,1:T(8,128)(2,1)}) %all-gather.13.cloned.1.call-update) | async-done | bytes 1638416 | tf_op jit(solution)/shard_map/all_gather | solution.py:23
  312.7 17.7 %reduce-scatter.23.cloned.1.call-done = f32[512,1600]{0,1:T(8,128)} async-done(((f32[1024,1600]{0,1:T(8,128)}), f32[512,1600]{0,1:T(8,128)}) %reduce-scatter.23.cloned.1.call-update) | async-done | bytes 3276816 | tf_op jit(solution)/shard_map/reduce_scatter | solution.py:27
  337.5 13.0 %all-gather.19.cloned.1.call-done = bf16[1024,1600]{0,1:T(8,128)(2,1)} async-done(((bf16[512,1600]{0,1:T(8,128)(2,1)}), bf16[1024,1600]{0,1:T(8,128)(2,1)}) %all-gather.19.cloned.1.call-update) | async-done | bytes 3276816 | tf_op jit(solution)/shard_map/all_gather | solution.py:31
  372.9 41.4 %reduce-scatter.29.cloned.1.call-done = f32[256,800]{0,1:T(8,128)} async-done(((f32[1024,800]{0,1:T(8,128)}), f32[256,800]{0,1:T(8,128)}) %reduce-scatter.29.cloned.1.call-update) | async-done | bytes 819216 | tf_op jit(solution)/shard_map/reduce_scatter | solution.py:35
  418.5 43.8 %reduce-scatter.25.cloned.1.call-done = f32[256,800]{0,1:T(8,128)} async-done(((f32[1024,800]{0,1:T(8,128)}), f32[256,800]{0,1:T(8,128)}) %reduce-scatter.25.cloned.1.call-update) | async-done | bytes 819216 | tf_op jit(solution)/shard_map/reduce_scatter | solution.py:35
  465.9 31.4 %all-gather.21.cloned.1.call-done = bf16[1024,800]{0,1:T(8,128)(2,1)} async-done(((bf16[256,800]{0,1:T(8,128)(2,1)}), bf16[1024,800]{0,1:T(8,128)(2,1)}) %all-gather.21.cloned.1.call-update) | async-done | bytes 1638416 | tf_op jit(solution)/shard_map/all_gather | solution.py:23
  500.9 9.5 reduce-scatter.31.cloned.1.call-done
  523.2 52.5 %while.29 = (s32[]{:T(128)}, f32[5,128,5,64]{1,3,2,0:T(8,128)S(1)}, bf16[5,1024,5,64]{1,3,2,0:T(8,128)(2,1)}, bf16[5,1024,5,64]{1,3,2,0:T(8,128)(2,1)}, bf16[5,1...) while((s32[]{:T(128)}, f32[5,128,5,64]{1,3,2,0:T(8,128)S(1)}, ...), condition=%wide.region_25.26_spmd.clone, body=%wide.region_23.25_spmd.clone.sunk | while | flops 426909056 | bytes 17467036 | solution.py:142
  591.8 63.0 %reduce-scatter.39.cloned.1.call-done = bf16[128,3200]{1,0:T(8,128)(2,1)} async-done(((bf16[1024,3200]{1,0:T(8,128)(2,1)}), bf16[128,3200]{1,0:T(8,128)(2,1)}) %reduce-scatter.39.cloned.1.call-update) | async-done | bytes 819216
  656.7 18.8 %all_to_all.72 = bf16[128,4,1200]{0,2,1:T(8,128)(2,1)S(1)} all-to-all(bf16[128,4,1200]{0,2,1:T(8,128)(2,1)S(1)} %bitcast.226), channel_id=1, replica_groups=mesh['dp'=4,'row'=4,'col'=2] {'row'}, dimensions={1} | all-to-all | bytes 2457600 | tf_op jit(solution)/shard_map/all_to_all | solution.py:43
  707.7 35.1 %reduce-scatter.41.cloned.1.call-done = bf16[200,1600]{1,0:T(8,128)(2,1)} async-done(((bf16[800,1600]{1,0:T(8,128)(2,1)}), bf16[200,1600]{1,0:T(8,128)(2,1)}) %reduce-scatter.41.cloned.1.call-update) | async-done | bytes 640016
  747.6 36.1 %fusion.4 = bf16[112,800]{1,0:T(8,128)(2,1)S(1)} fusion(bf16[400,800]{1,0:T(8,128)(2,1)S(1)} %convolution_convert_fusion.3), kind=kCustom, calls=%all-reduce-scatter | all-reduce-scatter fusion | flops 358401 | bytes 819712
  788.3 25.3 %reduce-scatter.37.cloned.1.call-done = bf16[400,800]{1,0:T(8,128)(2,1)} async-done(((bf16[1600,800]{1,0:T(8,128)(2,1)}), bf16[400,800]{1,0:T(8,128)(2,1)}) %reduce-scatter.37.cloned.1.call-update) | async-done | bytes 640016 | tf_op jit(solution)/shard_map/reduce_scatter | solution.py:321
  820.5 39.6 %reduce-scatter.35.cloned.1.call-done = bf16[200,1200]{1,0:T(8,128)(2,1)} async-done(((bf16[800,1200]{1,0:T(8,128)(2,1)}), bf16[200,1200]{1,0:T(8,128)(2,1)}) %reduce-scatter.35.cloned.1.call-update) | async-done | bytes 480016 | tf_op jit(solution)/shard_map/reduce_scatter | solution.py:330
  862.3 45.7 %reduce-scatter.33.cloned.1.call-done = f32[256,800]{0,1:T(8,128)} async-done(((f32[1024,800]{0,1:T(8,128)}), f32[256,800]{0,1:T(8,128)}) %reduce-scatter.33.cloned.1.call-update) | async-done | bytes 819216 | tf_op jit(solution)/shard_map/reduce_scatter | solution.py:35
  915.9 128.6 %all-reduce.10.cloned.1.call-done = (f32[1600]{0:T(1024)}, f32[1600]{0:T(1024)}, f32[1600]{0:T(1024)}, f32[1600]{0:T(1024)}, f32[1600]{0:T(1024)}, /*index=5*/f3...) async-done(((f32[1600]{0:T(1024)}, f32[1600]{0:T(1024)}, f32[1600]{0:T(1024)}, f32[1600]{0:T(1024)}, f32[1600]{0:T(1024)}, /*index=5*/f32[1600]{0:T(1024)}, ...) | async-done | bytes 76816 | tf_op jit(solution)/shard_map/psum | solution.py:347
  (280 shorter events, 282.3 us)
Async XLA Ops:
  7.2 288.7 %copy-start = (bf16[800,1600]{1,0:T(8,128)(2,1)S(1)}, bf16[800,1600]{1,0:T(8,128)(2,1)}, u32[]{:S(2)}) copy-start(bf16[800,1600]{1,0:T(8,128)(2,1)} %param.31) | copy-start | bytes 7680004
  7.2 40.0 %all-gather.9.cloned.1.call-start = ((), (), s32[]{:S(2)}) async-start(), calls=%async_computation.16 | async-start | bytes 2048000 | tf_op jit(solution)/shard_map/all_gather | solution.py:23
  14.6 52.6 %reduce-scatter.19.cloned.1.call-start = ((), (), s32[]{:S(2)}) async-start(), calls=%async_computation.17 | async-start | bytes 7372800 | tf_op jit(solution)/shard_map/reduce_scatter | solution.py:27
  54.2 84.2 %all-gather.11.cloned.1.call-start = ((), (), s32[]{:S(2)}) async-start(), calls=%async_computation.18 | async-start | bytes 7372800 | tf_op jit(solution)/shard_map/all_gather | solution.py:47
  91.3 138.1 %reduce-scatter.21.cloned.1.call-start = ((), (), s32[]{:S(2)}) async-start(), calls=%async_computation.19 | async-start | bytes 4096000 | tf_op jit(solution)/shard_map/reduce_scatter | solution.py:35
  185.2 77.2 %all-gather.17.cloned.1.call-start = ((), (), s32[]{:S(2)}) async-start(), calls=%async_computation.24 | async-start | bytes 2048000 | tf_op jit(solution)/shard_map/all_gather | solution.py:23
  185.7 110.2 %all-gather.13.cloned.1.call-start = ((), (), s32[]{:S(2)}) async-start(), calls=%async_computation.20 | async-start | bytes 2048000 | tf_op jit(solution)/shard_map/all_gather | solution.py:23
  235.7 77.0 %reduce-scatter.27.cloned.1.call-start = ((), (), s32[]{:S(2)}) async-start(), calls=%async_computation.25 | async-start | bytes 9830400 | tf_op jit(solution)/shard_map/reduce_scatter | solution.py:27
  271.0 59.3 %reduce-scatter.23.cloned.1.call-start = ((), (), s32[]{:S(2)}) async-start(), calls=%async_computation.21 | async-start | bytes 9830400 | tf_op jit(solution)/shard_map/reduce_scatter | solution.py:27
  303.7 46.8 %all-gather.19.cloned.1.call-start = ((), (), s32[]{:S(2)}) async-start(), calls=%async_computation.26 | async-start | bytes 4915200 | tf_op jit(solution)/shard_map/all_gather | solution.py:31
  336.8 28.6 %all-gather.15.cloned.1.call-start = ((), (), s32[]{:S(2)}) async-start(), calls=%async_computation.22 | async-start | bytes 4915200 | tf_op jit(solution)/shard_map/all_gather | solution.py:31
  337.4 76.9 %reduce-scatter.29.cloned.1.call-start = ((), (), s32[]{:S(2)}) async-start(), calls=%async_computation.27 | async-start | bytes 4096000 | tf_op jit(solution)/shard_map/reduce_scatter | solution.py:35
  357.2 105.0 %reduce-scatter.25.cloned.1.call-start = ((), (), s32[]{:S(2)}) async-start(), calls=%async_computation.23 | async-start | bytes 4096000 | tf_op jit(solution)/shard_map/reduce_scatter | solution.py:35
  372.2 125.0 %all-gather.21.cloned.1.call-start = ((), (), s32[]{:S(2)}) async-start(), calls=%async_computation.28 | async-start | bytes 2048000 | tf_op jit(solution)/shard_map/all_gather | solution.py:23
  465.8 44.6 %reduce-scatter.31.cloned.1.call-start = ((), (), s32[]{:S(2)}) async-start(), calls=%async_computation.29 | async-start | bytes 2457600 | tf_op jit(solution)/shard_map/reduce_scatter | solution.py:27
  512.4 10.8 %all-to-all-start.2 = ((bf16[4,128,400]{1,2,0:T(8,128)(2,1)}), bf16[4,128,400]{1,2,0:T(8,128)(2,1)S(1)}, u32[]{:S(2)}, u32[]{:S(2)}) async-start(bf16[4,128,400]{1,2,0:T(8,128)(2,1)} %copy_bitcast_fusion.3), calls=%async_computation.9 | async-start | bytes 819200 | tf_op jit(solution)/shard_map/all_to_all | solution.py:39
  516.0 138.8 %reduce-scatter.39.cloned.1.call-start = ((), (), s32[]{:S(2)}) async-start(), calls=%async_computation.34 | async-start | bytes 7372800
  591.7 100.7 %all-gather.23.cloned.1.call-start = ((), (), s32[]{:S(2)}) async-start(), calls=%async_computation.30 | async-start | bytes 3686400 | tf_op jit(solution)/shard_map/all_gather | solution.py:31
  676.6 66.3 %reduce-scatter.41.cloned.1.call-start = ((), (), s32[]{:S(2)}) async-start(), calls=%async_computation.35 | async-start | bytes 3328000
  683.8 129.8 %reduce-scatter.37.cloned.1.call-start = ((), (), s32[]{:S(2)}) async-start(), calls=%async_computation.33 | async-start | bytes 3584000 | tf_op jit(solution)/shard_map/reduce_scatter | solution.py:321
  692.3 167.7 %reduce-scatter.35.cloned.1.call-start = ((), (), s32[]{:S(2)}) async-start(), calls=%async_computation.32 | async-start | bytes 2560000 | tf_op jit(solution)/shard_map/reduce_scatter | solution.py:330
  699.2 208.8 %reduce-scatter.33.cloned.1.call-start = ((), (), s32[]{:S(2)}) async-start(), calls=%async_computation.31 | async-start | bytes 4096000 | tf_op jit(solution)/shard_map/reduce_scatter | solution.py:35
  705.5 338.9 %all-reduce.10.cloned.1.call-start = ((), (), s32[]{:S(2)}) async-start(), calls=%async_computation.36 | async-start | bytes 188416 | tf_op jit(solution)/shard_map/psum | solution.py:347
  783.8 33.2 %collective-permute-start = (bf16[36,800]{1,0:T(8,128)(2,1)S(1)}, bf16[36,800]{1,0:T(8,128)(2,1)S(1)}, u32[]{:S(2)}, u32[]{:S(2)}) collective-permute-start(bf16[36,800]{1,0:T(8,128)(2,1)S(1)} %slice.31), channel_id=1, source_target_pairs={{0,8},{8,16},{16,24},{1,9},{9,17},{17,25},{2,10},{10,18},{18,26},{... | collective-permute-start | bytes 172808
  (34 other events, 1158.7 us)
Sparse Core Ops, SparseCore 0:
  14.7 32.3 all-gather.8
  54.3 12.8 reduce-scatter.18
  91.4 46.9 all-gather.10
  185.3 44.1 reduce-scatter.20
  231.1 31.2 all-gather.16
  264.6 31.2 all-gather.12
  298.2 14.4 reduce-scatter.26
  315.0 15.3 reduce-scatter.22
  337.0 13.4 all-gather.18
  351.9 13.4 all-gather.14
  368.4 45.8 reduce-scatter.28
  417.2 44.9 reduce-scatter.24
  465.9 31.2 all-gather.20
  501.0 9.3 reduce-scatter.30
  591.8 63.0 reduce-scatter.38
  676.7 10.5 all-gather.22
  689.5 53.3 reduce-scatter.40
  745.0 68.5 reduce-scatter.36
  815.9 44.0 reduce-scatter.34
  862.9 44.9 reduce-scatter.32
  915.5 128.8 all-reduce.9
where the time goes:
time: 1070 us; the launch traced here: 1060 us
  waiting for transfers between devices  704 us (66%)
  matrix products  136 us (13%)
  blocking collectives  98.6 us (9%)
  other arithmetic  51.1 us (5%)
  local copies, waits for them, and re-layouts  47.7 us (4%)
  between operations  15.6 us (1%)
    reduce_scatter x4, waiting for transfers between devices, reduce_rows(): return lax.psum_scatter(partial_sum, 'row', scatter_dimension=0, tiled=True)  174 us
    psum x1, waiting for transfers between devices, shards(): lax.psum((col_place(first_gain_part), col_place(first_shift_part), query_...  129 us
    all_gather x4, waiting for transfers between devices, spread_rows(): return lax.all_gather(own_part, 'row', axis=0, tiled=True)  115 us
    unnamed x24, waiting for transfers between devices  99.6 us
    reduce_scatter x4, waiting for transfers between devices, reduce_cols(): return lax.psum_scatter(partial_sum, 'col', scatter_dimension=0, tiled=True)  47.5 us
    all_gather x1, waiting for transfers between devices, gather_keys(): return lax.all_gather(own_part, ('row', 'col'), axis=0, tiled=True)  45.9 us
    reduce_scatter x1, waiting for transfers between devices, shards(): lax.psum_scatter(triple_grad.astype(jnp.bfloat16), 'dp', scatter_dimensio...  39.6 us
    unnamed x1, blocking collectives  36.1 us
  transfers between devices with their start and end apart: 23, of which 21 were waited for; matrix products, arithmetic and copies ran while one was open for 11% of the time, Pallas kernels for 0%

commit v1 on v0

--- a/solution.py
+++ b/solution.py
@@ -11,6 +11,22 @@
 NEG = -1e30
 
 
+def gather_around(x, axis, dim):
+    ways, here, step = (lax.axis_size(axis), lax.axis_index(axis), x.shape[dim])
+    shape = [n * ways if d == dim else n for d, n in enumerate(x.shape)]
+    full = lax.dynamic_update_slice_in_dim(jnp.zeros(shape, x.dtype), x, here * step, axis=dim)
+    going_up = going_down = x
+    for far in range(1, ways // 2 + 1):
+        going_up = lax.ppermute(going_up, axis, [(d, (d + 1) % ways) for d in range(ways)])
+        full = lax.dynamic_update_slice_in_dim(full, going_up, (here - far) % ways * step, axis=dim)
+        if 2 * far < ways:
+            going_down = lax.ppermute(going_down, axis, [(d, (d - 1) % ways) for d in range(ways)])
+            full = lax.dynamic_update_slice_in_dim(
+                full, going_down, (here + far) % ways * step, axis=dim
+            )
+    return full
+
+
 def gelu_tanh(values):
     return (
         0.5
@@ -20,7 +36,7 @@
 
 
 def spread_rows(own_part):
-    return lax.all_gather(own_part, "row", axis=0, tiled=True)
+    return gather_around(own_part, "row", 0)
 
 
 def reduce_cols(partial_sum):

time: 1070 us -> 1050 us (0.981)
  waiting for transfers between devices: 704 us -> 658 us
  starting transfers between devices: 9.8 us -> 24.7 us
    ppermute x0 -> x12, waiting for transfers between devices: none -> 120 us  [the longest x8 80.1 us: gather_around(): lax.ppermute(going_up, axis, [(d, (d + 1) % ways) for d in range(ways)])]
    all_gather x4 -> x0, waiting for transfers between devices: 115 us -> none  [spread_rows(): return lax.all_gather(own_part, 'row', axis=0, tiled=True)]
    reduce_scatter x4, waiting for transfers between devices: 174 us -> 137 us  [reduce_rows(): return lax.psum_scatter(partial_sum, 'row', scatter_dimension=0, tiled=True)]
    ppermute x0 -> x12, starting transfers between devices: none -> 13.6 us  [the longest x8 6.93 us: gather_around(): lax.ppermute(going_up, axis, [(d, (d + 1) % ways) for d in range(ways)])]
    reduce_scatter x4, waiting for transfers between devices: 47.5 us -> 35.8 us  [reduce_cols(): return lax.psum_scatter(partial_sum, 'col', scatter_dimension=0, tiled=True)]
    unnamed x85 -> x91, local copies, waits for them, and re-layouts: 32.7 us -> 35.4 us
    unnamed x24 -> x20, waiting for transfers between devices: 99.6 us -> 98.9 us
  transfers between devices with their start and end apart: 23 -> 31, of which waited for: 21 -> 28; matrix products, arithmetic and copies ran while one was open for 11% -> 11% of each run, Pallas kernels for 0% -> 0%
where the time goes in v1:
time: 1050 us; the launch traced here: 1040 us
  waiting for transfers between devices  658 us (63%)
  matrix products  133 us (13%)
  blocking collectives  97.7 us (9%)
  local copies, waits for them, and re-layouts  57.6 us (5%)
  other arithmetic  51.5 us (5%)
  starting transfers between devices  24.7 us (2%)
  between operations  15.4 us (1%)
    reduce_scatter x4, waiting for transfers between devices, reduce_rows(): return lax.psum_scatter(partial_sum, 'row', scatter_dimension=0, tiled=True)  137 us
    psum x1, waiting for transfers between devices, shards(): lax.psum((col_place(first_gain_part), col_place(first_shift_part), query_...  128 us
    unnamed x20, waiting for transfers between devices  98.9 us
    ppermute x8, waiting for transfers between devices, gather_around(): lax.ppermute(going_up, axis, [(d, (d + 1) % ways) for d in range(ways)])  80.1 us
    all_gather x1, waiting for transfers between devices, gather_keys(): return lax.all_gather(own_part, ('row', 'col'), axis=0, tiled=True)  45.9 us
    ppermute x4, waiting for transfers between devices, gather_around(): lax.ppermute(going_down, axis, [(d, (d - 1) % ways) for d in range(ways)])  40.3 us
    reduce_scatter x1, waiting for transfers between devices, shards(): lax.psum_scatter(triple_grad.astype(jnp.bfloat16), 'dp', scatter_dimensio...  38.3 us
    reduce_scatter x4, waiting for transfers between devices, reduce_cols(): return lax.psum_scatter(partial_sum, 'col', scatter_dimension=0, tiled=True)  35.8 us
  transfers between devices with their start and end apart: 31, of which 28 were waited for; matrix products, arithmetic and copies ran while one was open for 11% of the time, Pallas kernels for 0%

profile of v1, /device:TPU:8, one launch (start us, length us, event | category | flops | bytes accessed | tf_op | source)
XLA Modules:
  0.0 1038.0 jit_solution(7015702033414544385)
XLA Ops:
  19.0 10.3 collective-permute-done
  55.9 12.5 %reduce-scatter.19.cloned.1.call-done = f32[512,1200]{0,1:T(8,128)} async-done(((f32[1024,1200]{0,1:T(8,128)}), f32[512,1200]{0,1:T(8,128)}) %reduce-scatter.19.cloned.1.call-update) | async-done | bytes 2457616 | tf_op jit(solution)/shard_map/reduce_scatter | solution.py:43
  70.3 20.1 %all_to_all.70 = bf16[4,128,1200]{1,2,0:T(8,128)(2,1)S(1)} all-to-all(bf16[4,128,1200]{1,2,0:T(8,128)(2,1)S(1)} %copy_bitcast_fusion.1), channel_id=1, replica_groups=mesh['dp'=4,'row'=4,'col'=2] {'row'}, dimensions={0} | all-to-all | bytes 2457600 | tf_op jit(solution)/shard_map/all_to_all | solution.py:55
  93.6 45.9 %all-gather.5.cloned.1.call-done = bf16[1024,3200]{0,1:T(8,128)(2,1)} async-done(((bf16[128,3200]{0,1:T(8,128)(2,1)}), bf16[1024,3200]{0,1:T(8,128)(2,1)}) %all-gather.5.cloned.1.call-update) | async-done | bytes 6553616 | tf_op jit(solution)/shard_map/all_gather | solution.py:63
  146.0 23.4 %while.28 = (s32[]{:T(128)}, bf16[5,128,5,64]{1,3,2,0:T(8,128)(2,1)S(1)}, f32[5,5,128]{2,1,0:T(8,128)S(1)}, bf16[5,1024,5,64]{1,3,2,0:T(8,128)(2,1)}, bf16[5,128...) while((s32[]{:T(128)}, ...), condition=%wide.region_8.9_spmd.clone, body=%wide.region_5.8_spmd.clone.sunk | while | flops 175414656 | bytes 9902705 | solution.py:118
  169.5 10.8 %all_to_all.71 = bf16[128,4,400]{0,2,1:T(8,128)(2,1)S(1)} all-to-all(bf16[128,4,400]{0,2,1:T(8,128)(2,1)S(1)} %bitcast.232), channel_id=1, replica_groups=mesh['dp'=4,'row'=4,'col'=2] {'row'}, dimensions={1} | all-to-all | bytes 819200 | tf_op jit(solution)/shard_map/all_to_all | solution.py:59
  190.3 15.8 %collective-permute-done.6 = bf16[256,800]{0,1:T(8,128)(2,1)S(1)} collective-permute-done((bf16[256,800]{0,1:T(8,128)(2,1)S(1)}, bf16[256,800]{0,1:T(8,128)(2,1)S(1)}, u32[]{:S(2)}, u32[]{:S(2)}) %collective-permute-start.6) | collective-permute-done | bytes 409632 | tf_op jit(solution)/shard_map/ppermute | solution.py:20
  206.3 16.4 %collective-permute-done.7 = bf16[256,800]{0,1:T(8,128)(2,1)S(1)} collective-permute-done((bf16[256,800]{0,1:T(8,128)(2,1)S(1)}, bf16[256,800]{0,1:T(8,128)(2,1)S(1)}, u32[]{:S(2)}, u32[]{:S(2)}) %collective-permute-start.7) | collective-permute-done | bytes 409632 | tf_op jit(solution)/shard_map/ppermute | solution.py:23
  222.8 12.0 %collective-permute-done.8 = bf16[256,800]{0,1:T(8,128)(2,1)S(1)} collective-permute-done((bf16[256,800]{0,1:T(8,128)(2,1)S(1)}, bf16[256,800]{0,1:T(8,128)(2,1)S(1)}, u32[]{:S(2)}, u32[]{:S(2)}) %collective-permute-start.8) | collective-permute-done | bytes 409632 | tf_op jit(solution)/shard_map/ppermute | solution.py:20
  257.4 10.3 collective-permute-done.3
  292.2 13.8 %reduce-scatter.23.cloned.1.call-done = f32[512,1600]{0,1:T(8,128)} async-done(((f32[1024,1600]{0,1:T(8,128)}), f32[512,1600]{0,1:T(8,128)}) %reduce-scatter.23.cloned.1.call-update) | async-done | bytes 3276816 | tf_op jit(solution)/shard_map/reduce_scatter | solution.py:43
  313.3 12.8 %all-gather.9.cloned.1.call-done = bf16[1024,1600]{0,1:T(8,128)(2,1)} async-done(((bf16[512,1600]{0,1:T(8,128)(2,1)}), bf16[1024,1600]{0,1:T(8,128)(2,1)}) %all-gather.9.cloned.1.call-update) | async-done | bytes 3276816 | tf_op jit(solution)/shard_map/all_gather | solution.py:47
  348.8 41.3 %reduce-scatter.29.cloned.1.call-done = f32[256,800]{0,1:T(8,128)} async-done(((f32[1024,800]{0,1:T(8,128)}), f32[256,800]{0,1:T(8,128)}) %reduce-scatter.29.cloned.1.call-update) | async-done | bytes 819216 | tf_op jit(solution)/shard_map/reduce_scatter | solution.py:51
  394.2 43.9 %reduce-scatter.25.cloned.1.call-done = f32[256,800]{0,1:T(8,128)} async-done(((f32[1024,800]{0,1:T(8,128)}), f32[256,800]{0,1:T(8,128)}) %reduce-scatter.25.cloned.1.call-update) | async-done | bytes 819216 | tf_op jit(solution)/shard_map/reduce_scatter | solution.py:51
  444.1 10.3 collective-permute-done.9
  495.3 55.7 %while.29 = (s32[]{:T(128)}, f32[5,128,5,64]{1,3,2,0:T(8,128)}, bf16[5,1024,5,64]{1,3,2,0:T(8,128)(2,1)}, bf16[5,1024,5,64]{1,3,2,0:T(8,128)(2,1)}, bf16[5,1024,...) while((s32[]{:T(128)}, f32[5,128,5,64]{1,3,2,0:T(8,128)}, ...), condition=%wide.region_25.26_spmd.clone, body=%wide.region_23.25_spmd.clone.sunk | while | flops 426909056 | bytes 17467028 | solution.py:158
  568.2 61.9 %reduce-scatter.39.cloned.1.call-done = bf16[128,3200]{1,0:T(8,128)(2,1)} async-done(((bf16[1024,3200]{1,0:T(8,128)(2,1)}), bf16[128,3200]{1,0:T(8,128)(2,1)}) %reduce-scatter.39.cloned.1.call-update) | async-done | bytes 819216
  631.9 18.8 %all_to_all.72 = bf16[128,4,1200]{0,2,1:T(8,128)(2,1)S(1)} all-to-all(bf16[128,4,1200]{0,2,1:T(8,128)(2,1)S(1)} %bitcast.226), channel_id=1, replica_groups=mesh['dp'=4,'row'=4,'col'=2] {'row'}, dimensions={1} | all-to-all | bytes 2457600 | tf_op jit(solution)/shard_map/all_to_all | solution.py:59
  682.2 36.1 %reduce-scatter.41.cloned.1.call-done = bf16[200,1600]{1,0:T(8,128)(2,1)} async-done(((bf16[800,1600]{1,0:T(8,128)(2,1)}), bf16[200,1600]{1,0:T(8,128)(2,1)}) %reduce-scatter.41.cloned.1.call-update) | async-done | bytes 640016
  722.4 34.7 %fusion.4 = bf16[112,800]{1,0:T(8,128)(2,1)S(1)} fusion(bf16[400,800]{1,0:T(8,128)(2,1)} %convolution_convert_fusion.3), kind=kCustom, calls=%all-reduce-scatter | all-reduce-scatter fusion | flops 358401 | bytes 819712
  763.6 25.3 %reduce-scatter.37.cloned.1.call-done = bf16[400,800]{1,0:T(8,128)(2,1)} async-done(((bf16[1600,800]{1,0:T(8,128)(2,1)}), bf16[400,800]{1,0:T(8,128)(2,1)}) %reduce-scatter.37.cloned.1.call-update) | async-done | bytes 640016 | tf_op jit(solution)/shard_map/reduce_scatter | solution.py:337
  797.0 38.3 %reduce-scatter.35.cloned.1.call-done = bf16[200,1200]{1,0:T(8,128)(2,1)} async-done(((bf16[800,1200]{1,0:T(8,128)(2,1)}), bf16[200,1200]{1,0:T(8,128)(2,1)}) %reduce-scatter.35.cloned.1.call-update) | async-done | bytes 480016 | tf_op jit(solution)/shard_map/reduce_scatter | solution.py:346
  837.5 45.7 %reduce-scatter.33.cloned.1.call-done = f32[256,800]{0,1:T(8,128)} async-done(((f32[1024,800]{0,1:T(8,128)}), f32[256,800]{0,1:T(8,128)}) %reduce-scatter.33.cloned.1.call-update) | async-done | bytes 819216 | tf_op jit(solution)/shard_map/reduce_scatter | solution.py:51
  891.1 128.4 %all-reduce.10.cloned.1.call-done = (f32[1600]{0:T(1024)}, f32[1600]{0:T(1024)}, f32[1600]{0:T(1024)}, f32[1600]{0:T(1024)}, f32[1600]{0:T(1024)}, /*index=5*/f3...) async-done(((f32[1600]{0:T(1024)}, f32[1600]{0:T(1024)}, f32[1600]{0:T(1024)}, f32[1600]{0:T(1024)}, f32[1600]{0:T(1024)}, /*index=5*/f32[1600]{0:T(1024)}, ...) | async-done | bytes 76816 | tf_op jit(solution)/shard_map/psum | solution.py:363
  (315 shorter events, 356.8 us)
Async XLA Ops:
  7.2 61.2 %reduce-scatter.19.cloned.1.call-start = ((), (), s32[]{:S(2)}) async-start(), calls=%async_computation.16 | async-start | bytes 7372800 | tf_op jit(solution)/shard_map/reduce_scatter | solution.py:43
  17.6 20.7 %collective-permute-start.1 = (bf16[256,800]{0,1:T(8,128)(2,1)S(1)}, bf16[256,800]{0,1:T(8,128)(2,1)}, u32[]{:S(2)}, u32[]{:S(2)}) collective-permute-start(bf16[256,800]{0,1:T(8,128)(2,1)S(1)} %get-tuple-element.326), channel_id=1, source_target_pairs={{0,6},{2,0},{4,2},{6,4},{1,7},{3,1},{5,3},{7,5},{8,14},{10,8},{12,... | collective-permute-start | bytes 1228808 | tf_op jit(solution)/shard_map/ppermute | solution.py:23
  55.1 84.4 %all-gather.5.cloned.1.call-start = ((), (), s32[]{:S(2)}) async-start(), calls=%async_computation.17 | async-start | bytes 7372800 | tf_op jit(solution)/shard_map/all_gather | solution.py:63
  92.4 155.9 %reduce-scatter.21.cloned.1.call-start = ((), (), s32[]{:S(2)}) async-start(), calls=%async_computation.18 | async-start | bytes 4096000 | tf_op jit(solution)/shard_map/reduce_scatter | solution.py:51
  186.4 105.8 %reduce-scatter.27.cloned.1.call-start = ((), (), s32[]{:S(2)}) async-start(), calls=%async_computation.22 | async-start | bytes 9830400 | tf_op jit(solution)/shard_map/reduce_scatter | solution.py:43
  187.3 18.7 %collective-permute-start.6 = (bf16[256,800]{0,1:T(8,128)(2,1)S(1)}, bf16[256,800]{0,1:T(8,128)(2,1)S(1)}, u32[]{:S(2)}, u32[]{:S(2)}) collective-permute-start(bf16[256,800]{0,1:T(8,128)(2,1)S(1)} %copy-done.6), channel_id=1, source_target_pairs={{0,2},{2,4},{4,6},{6,0},{1,3},{3,5},{5,7},{7,1},{8,10},{10,12},{12... | collective-permute-start | bytes 1228808 | tf_op jit(solution)/shard_map/ppermute | solution.py:20
  187.9 34.8 %collective-permute-start.7 = (bf16[256,800]{0,1:T(8,128)(2,1)S(1)}, bf16[256,800]{0,1:T(8,128)(2,1)S(1)}, u32[]{:S(2)}, u32[]{:S(2)}) collective-permute-start(bf16[256,800]{0,1:T(8,128)(2,1)S(1)} %copy-done.6), channel_id=1, source_target_pairs={{0,6},{2,0},{4,2},{6,4},{1,7},{3,1},{5,3},{7,5},{8,14},{10,8},{12,... | collective-permute-start | bytes 1228808 | tf_op jit(solution)/shard_map/ppermute | solution.py:23
  206.0 28.8 %collective-permute-start.8 = (bf16[256,800]{0,1:T(8,128)(2,1)S(1)}, bf16[256,800]{0,1:T(8,128)(2,1)S(1)}, u32[]{:S(2)}, u32[]{:S(2)}) collective-permute-start(bf16[256,800]{0,1:T(8,128)(2,1)S(1)} %collective-permute-done.6), channel_id=1, source_target_pairs={{0,2},{2,4},{4,6},{6,0},{1,3},{3,5},{5,7},{7,1},{8,10},{10,12},{12... | collective-permute-start | bytes 1228808 | tf_op jit(solution)/shard_map/ppermute | solution.py:20
  241.7 64.2 %reduce-scatter.23.cloned.1.call-start = ((), (), s32[]{:S(2)}) async-start(), calls=%async_computation.19 | async-start | bytes 9830400 | tf_op jit(solution)/shard_map/reduce_scatter | solution.py:43
  256.0 20.6 %collective-permute-start.4 = (bf16[256,800]{0,1:T(8,128)(2,1)S(1)}, bf16[256,800]{0,1:T(8,128)(2,1)S(1)}, u32[]{:S(2)}, u32[]{:S(2)}) collective-permute-start(bf16[256,800]{0,1:T(8,128)(2,1)S(1)} %get-tuple-element.323), channel_id=1, source_target_pairs={{0,6},{2,0},{4,2},{6,4},{1,7},{3,1},{5,3},{7,5},{8,14},{10,8},{12,... | collective-permute-start | bytes 1228808 | tf_op jit(solution)/shard_map/ppermute | solution.py:23
  291.4 34.8 %all-gather.9.cloned.1.call-start = ((), (), s32[]{:S(2)}) async-start(), calls=%async_computation.23 | async-start | bytes 4915200 | tf_op jit(solution)/shard_map/all_gather | solution.py:47
  312.5 28.7 %all-gather.7.cloned.1.call-start = ((), (), s32[]{:S(2)}) async-start(), calls=%async_computation.20 | async-start | bytes 4915200 | tf_op jit(solution)/shard_map/all_gather | solution.py:47
  313.2 76.9 %reduce-scatter.29.cloned.1.call-start = ((), (), s32[]{:S(2)}) async-start(), calls=%async_computation.24 | async-start | bytes 4096000 | tf_op jit(solution)/shard_map/reduce_scatter | solution.py:51
  332.9 105.3 %reduce-scatter.25.cloned.1.call-start = ((), (), s32[]{:S(2)}) async-start(), calls=%async_computation.21 | async-start | bytes 4096000 | tf_op jit(solution)/shard_map/reduce_scatter | solution.py:51
  348.0 134.4 %reduce-scatter.31.cloned.1.call-start = ((), (), s32[]{:S(2)}) async-start(), calls=%async_computation.25 | async-start | bytes 2457600 | tf_op jit(solution)/shard_map/reduce_scatter | solution.py:43
  442.6 20.5 %collective-permute-start.10 = (bf16[256,800]{0,1:T(8,128)(2,1)S(1)}, bf16[256,800]{0,1:T(8,128)(2,1)S(1)}, u32[]{:S(2)}, u32[]{:S(2)}) collective-permute-start(bf16[256,800]{0,1:T(8,128)(2,1)S(1)} %get-tuple-element.321), channel_id=1, source_target_pairs={{0,6},{2,0},{4,2},{6,4},{1,7},{3,1},{5,3},{7,5},{8,14},{10,8},{12,... | collective-permute-start | bytes 1228808 | tf_op jit(solution)/shard_map/ppermute | solution.py:23
  488.1 142.0 %reduce-scatter.39.cloned.1.call-start = ((), (), s32[]{:S(2)}) async-start(), calls=%async_computation.30 | async-start | bytes 7372800
  566.9 100.8 %all-gather.11.cloned.1.call-start = ((), (), s32[]{:S(2)}) async-start(), calls=%async_computation.26 | async-start | bytes 3686400 | tf_op jit(solution)/shard_map/all_gather | solution.py:47
  651.8 66.4 %reduce-scatter.41.cloned.1.call-start = ((), (), s32[]{:S(2)}) async-start(), calls=%async_computation.31 | async-start | bytes 3328000
  659.0 129.9 %reduce-scatter.37.cloned.1.call-start = ((), (), s32[]{:S(2)}) async-start(), calls=%async_computation.29 | async-start | bytes 3584000 | tf_op jit(solution)/shard_map/reduce_scatter | solution.py:337
  667.7 167.6 %reduce-scatter.35.cloned.1.call-start = ((), (), s32[]{:S(2)}) async-start(), calls=%async_computation.28 | async-start | bytes 2560000 | tf_op jit(solution)/shard_map/reduce_scatter | solution.py:346
  673.7 209.5 %reduce-scatter.33.cloned.1.call-start = ((), (), s32[]{:S(2)}) async-start(), calls=%async_computation.27 | async-start | bytes 4096000 | tf_op jit(solution)/shard_map/reduce_scatter | solution.py:51
  680.0 339.5 %all-reduce.10.cloned.1.call-start = ((), (), s32[]{:S(2)}) async-start(), calls=%async_computation.32 | async-start | bytes 188416 | tf_op jit(solution)/shard_map/psum | solution.py:363
  757.1 35.2 %collective-permute-start.12 = (bf16[36,800]{1,0:T(8,128)(2,1)S(1)}, bf16[36,800]{1,0:T(8,128)(2,1)S(1)}, u32[]{:S(2)}, u32[]{:S(2)}) collective-permute-start(bf16[36,800]{1,0:T(8,128)(2,1)S(1)} %slice.31), channel_id=1, source_target_pairs={{0,8},{8,16},{16,24},{1,9},{9,17},{17,25},{2,10},{10,18},{18,26},{... | collective-permute-start | bytes 172808
  (45 other events, 1543.2 us)
Sparse Core Ops, SparseCore 0:
  55.2 13.1 reduce-scatter.18
  92.5 46.9 all-gather.4
  186.5 61.7 reduce-scatter.20
  250.4 14.4 reduce-scatter.26
  291.5 14.4 reduce-scatter.22
  312.6 13.4 all-gather.8
  327.7 13.4 all-gather.6
  344.2 45.8 reduce-scatter.28
  393.1 44.9 reduce-scatter.24
  473.1 9.3 reduce-scatter.30
  567.1 62.9 reduce-scatter.38
  652.0 10.6 all-gather.10
  664.9 53.3 reduce-scatter.40
  720.4 68.4 reduce-scatter.36
  791.1 44.0 reduce-scatter.34
  838.1 45.0 reduce-scatter.32
  890.6 128.8 all-reduce.9
